TPU v7x, 32 devices: a whole 2x2x4 slice. The times are simulated.
32 devices in a mesh: dp: 8 (over y, x, core), mp: 4 (over z).
Axes of the slice: x: 2, y: 2, z: 4, core: 2. Of those that a mesh axis runs over, the one named last changes fastest.
Arguments:
- tokens: bfloat16 [4096, 1024], P('dp', 'mp'), may hold values from -150 to 150
- pre_gain: bfloat16 [1024], P('mp'), may hold values from 0.25 to 1.75
- input_weight: bfloat16 [3, 1024, 1024], P(None, 'dp', 'mp'), may hold values from -0.125 to 0.125
- output_weight: bfloat16 [1024, 1024], P('mp', 'dp'), may hold values from -1 to 1
- position_bias: bfloat16 [16, 512, 512], P('mp'), may hold values from -3 to 353
- post_gain: bfloat16 [1024], P('mp'), may hold values from 0.25 to 1.75
Outputs:
- stream: bfloat16 [4096, 1024], P('dp', 'mp')
- normed: bfloat16 [4096, 1024], P('dp', 'mp')
All inputs are finite; a program needn't handle non-finite values.
Results may differ from a plain program's by a relative error of at most 0.013.
Values may be sent and summed in bfloat16 or wider, within the bound.
A program may use at most 64 MiB of HBM per device.

v0:
```python
import jax
import jax.numpy as jnp
from jax import lax
from jax.sharding import PartitionSpec as P

epsilon = 1e-06


def attend_all(mixed_heads, position_bias):
    row_count = mixed_heads.shape[1]
    inner_width = mixed_heads.shape[2]
    head_count = position_bias.shape[0]
    seq_len = position_bias.shape[1]
    grouped = mixed_heads.reshape(
        3, row_count // seq_len, seq_len, head_count, inner_width // head_count
    )
    bias_wide = position_bias.astype(jnp.float32)

    def one_sequence(sequence):
        sequence_block = lax.dynamic_index_in_dim(grouped, sequence, 1, keepdims=False)
        scores = (
            jnp.einsum(
                "qhd,khd->hqk",
                sequence_block[0],
                sequence_block[1],
                preferred_element_type=jnp.float32,
            )
            + bias_wide
        )
        row_max = jnp.max(scores, axis=2, keepdims=True)
        weights = jnp.exp(scores - row_max)
        probabilities = (weights / jnp.sum(weights, axis=2, keepdims=True)).astype(jnp.bfloat16)
        context = jnp.einsum(
            "hqk,khd->qhd", probabilities, sequence_block[2], preferred_element_type=jnp.float32
        )
        return context.reshape(seq_len, inner_width).astype(jnp.bfloat16)

    stacked = lax.map(one_sequence, jnp.arange(row_count // seq_len, dtype=jnp.int32))
    return stacked.reshape(row_count, inner_width)


def on_device(tokens, pre_gain, input_weight, output_weight, position_bias, post_gain):
    rows_all, gain_all = (
        lax.all_gather(tokens, "mp", axis=1, tiled=True),
        lax.all_gather(pre_gain, "mp", axis=0, tiled=True),
    )
    widened = rows_all.astype(jnp.float32)
    inverse_rms = lax.rsqrt(jnp.mean(widened * widened, axis=1, keepdims=True) + epsilon)
    normed_in = (widened * inverse_rms * gain_all.astype(jnp.float32)).astype(jnp.bfloat16)
    feature_count = tokens.shape[1]
    projected = jnp.einsum(
        "td,kdi->kti",
        normed_in,
        lax.all_gather(input_weight, "dp", axis=1, tiled=True),
        preferred_element_type=jnp.float32,
    )
    context = attend_all(projected.astype(jnp.bfloat16), position_bias)
    partial_value = jnp.dot(
        context,
        lax.all_gather(output_weight, "dp", axis=1, tiled=True),
        preferred_element_type=jnp.float32,
    )
    attention_out = lax.psum_scatter(
        partial_value.astype(jnp.bfloat16), "mp", scatter_dimension=1, tiled=True
    ).astype(jnp.float32)
    stream = (tokens.astype(jnp.float32) + attention_out).astype(jnp.bfloat16)
    restored = lax.optimization_barrier(stream).astype(jnp.float32)
    squares = lax.psum(jnp.sum(restored * restored, axis=1), "mp")
    post_rms = lax.rsqrt(squares[:, None] / (feature_count * lax.axis_size("mp")) + epsilon)
    normed = (restored * post_rms * post_gain.astype(jnp.float32)).astype(jnp.bfloat16)
    return (stream, normed)


def solution(mesh):
    return jax.shard_map(
        on_device,
        mesh=mesh,
        in_specs=(
            P("dp", "mp"),
            P("mp"),
            P(None, "dp", "mp"),
            P("mp", "dp"),
            P("mp", None, None),
            P("mp"),
        ),
        out_specs=(P("dp", "mp"), P("dp", "mp")),
        check_vma=False,
    )
```

profile of v0, /device:TPU:0, one launch (start us, length us, event | category | flops | bytes accessed | tf_op | source)
XLA Modules:
  0.0 123.4 jit_solution(2190378064825369234)
XLA Ops:
  7.2 0.0 all-gather.4.cloned.1.call-start
  7.2 0.7 all-gather.4.cloned.1.call-update
  7.9 0.0 all-gather.6.cloned.1.call-start
  7.9 1.7 %copy.11 = bf16[3,128,256]{1,2,0:T(8,128)(2,1)} copy(bf16[3,128,256]{2,1,0:T(8,128)(2,1)} %param.8) | data formatting | bytes 393216 | tf_op args[2]
  9.7 0.0 all-gather.6.cloned.1.call-update
  9.7 0.0 reduce-scatter.2.cloned.1.call-start
  9.8 0.7 reshape.34
  10.4 12.6 %all-gather = bf16[4,1,256]{2,1,0:T(2,128)(2,1)S(1)} all-gather(bf16[1,1,256]{2,1,0:T(2,128)(2,1)S(1)} %reshape.34), channel_id=1, replica_groups=mesh['dp'=8,'mp'=4] {'mp'}, dimensions={0}, use_global_device_ids=true | all-gather | bytes 2560 | tf_op jit(solution)/shard_map/all_gather | solution.py:45
  23.1 0.0 copy-start.2
  23.1 2.8 %copy.12 = bf16[4,512,512]{1,2,0:T(8,128)(2,1)S(1)} copy(bf16[4,512,512]{2,1,0:T(8,128)(2,1)} %param.10) | data formatting | bytes 4194304 | tf_op args[4]
  25.9 0.0 copy-done.2
  25.9 10.0 %all_gather.15 = bf16[256,1024]{1,0:T(8,128)(2,1)S(1)} all-gather(bf16[256,128]{1,0:T(8,128)(2,1)S(1)} %copy-done.2), channel_id=1, replica_groups=mesh['dp'=8,'mp'=4] {'dp'}, dimensions={1}, use_global_device_ids=true | all-gather | bytes 589824 | tf_op jit(solution)/shard_map/all_gather | solution.py:60
  35.9 6.2 %all-gather.4.cloned.1.call-done = bf16[512,1024]{1,0:T(8,128)(2,1)} async-done(((bf16[512,256]{1,0:T(8,128)(2,1)}), bf16[512,1024]{1,0:T(8,128)(2,1)}) %all-gather.4.cloned.1.call-update) | async-done | bytes 1048592 | tf_op jit(solution)/shard_map/all_gather | solution.py:44
  42.1 1.5 %fusion.2 = f32[512]{0:T(512)S(1)} fusion(bf16[512,1024]{1,0:T(8,128)(2,1)} %all-gather.4.cloned.1.call-done), kind=kLoop, calls=%fused_computation.7 | loop fusion | flops 1572352 | bytes 1050624 | tf_op jit(solution)/shard_map/reduce_sum | solution.py:48
  43.6 25.1 %all-gather.6.cloned.1.call-done = bf16[3,1024,256]{1,2,0:T(8,128)(2,1)} async-done(((bf16[3,128,256]{1,2,0:T(8,128)(2,1)}), bf16[3,1024,256]{1,2,0:T(8,128)(2,1)}) %all-gather.6.cloned.1.call-update) | async-done | bytes 1572880 | tf_op jit(solution)/shard_map/all_gather | solution.py:54
  68.7 2.8 %fusion.6 = bf16[3,512,256]{1,2,0:T(8,128)(2,1)S(1)} fusion(bf16[3,1024,256]{1,2,0:T(8,128)(2,1)} %all-gather.6.cloned.1.call-done, bf16[512,1024]{1,0:T(8,128)(2,1)} %all-gather.4.cloned.1.call-done, f32[1024]{0:T(1024)S(1)} %bitcast.26, f32[512]{0:T(512)S(1)} %add_rsqrt_fusion.1), kind=kOutput, calls=%fused_computation.13 | convolution fusion | flops 807796736 | bytes 3414016 | tf_op jit(solution)/shard_map/td,kdi->kti/dot_general | solution.py:51
  71.5 0.8 fusion.18
  72.3 1.5 %fusion.19 = f32[4,512]{1,0:T(4,128)S(1)} fusion(bf16[4,512,512]{1,2,0:T(8,128)(2,1)S(1)} %copy.12, bf16[512,4,64]{0,2,1:T(8,128)(2,1)S(1)} %bitcast.23, bf16[512,4,64]{0,2,1:T(8,128)(2,1)S(1)} %bitcast.21), kind=kOutput, calls=%fused_computation.29 | convolution fusion | flops 138412544 | bytes 2629632 | tf_op jit(solution)/shard_map/while/body/eval_jaxpr/sub | solution.py:31
  73.8 2.9 %fusion.7 = bf16[4,64,512]{2,1,0:T(8,128)(2,1)S(1)} fusion(bf16[512,4,64]{0,2,1:T(8,128)(2,1)} %bitcast.25, f32[4,512]{1,0:T(4,128)S(1)} %fusion.19, bf16[4,512,512]{1,2,0:T(8,128)(2,1)S(1)} %copy.12, bf16[512,4,64]{0,2,1:T(8,128)(2,1)S(1)} %bitcast.24, bf16[512,4,64]{0,2,1:T(8,128)(2,1)S(1)} %bitcast.22), kind=kOutput, calls=%fused_computation.14 | convolution fusion | flops 273811968 | bytes 3153920 | tf_op jit(solution)/shard_map/while/body/eval_jaxpr/hqk,khd->qhd/dot_general | solution.py:33
  76.6 0.0 copy-start.3
  76.6 0.0 copy-start.1
  76.6 1.4 %convolution_convert_fusion = bf16[512,1024]{1,0:T(8,128)(2,1)} fusion(bf16[512,256]{0,1:T(8,128)(2,1)S(1)} %bitcast.20, bf16[256,1024]{1,0:T(8,128)(2,1)S(1)} %all_gather.15), kind=kOutput, calls=%fused_computation.11 | convolution fusion | flops 268959744 | bytes 1835008 | tf_op jit(solution)/shard_map/dot_general | solution.py:58
  78.1 0.0 reduce-scatter.2.cloned.1.call-update
  78.1 0.0 copy-done.3
  78.1 27.4 %reduce-scatter.2.cloned.1.call-done = bf16[512,256]{1,0:T(8,128)(2,1)} async-done(((bf16[512,1024]{1,0:T(8,128)(2,1)}), bf16[512,256]{1,0:T(8,128)(2,1)}) %reduce-scatter.2.cloned.1.call-update) | async-done | bytes 262160 | tf_op jit(solution)/shard_map/reduce_scatter | solution.py:63
  105.6 0.0 copy-done.1
  105.6 1.0 add_convert_fusion
  106.6 0.0 copy-start
  106.6 0.1 fusion.12
  106.7 9.3 %psum.7 = f32[512]{0:T(512)S(1)} all-reduce(f32[512]{0:T(512)S(1)} %fusion.12), channel_id=1, replica_groups=mesh['dp'=8,'mp'=4] {'mp'}, use_global_device_ids=true, to_apply=%region_5.6 | all-reduce | flops 512 | bytes 4096 | tf_op jit(solution)/shard_map/psum | solution.py:68
  116.0 0.8 fusion.14
  116.9 0.0 copy-done
  (4 shorter events, 0.0 us)
Async XLA Ops:
  7.2 35.0 %all-gather.4.cloned.1.call-start = ((), (), s32[]{:S(2)}) async-start(), calls=%async_computation.1 | async-start | bytes 1310720 | tf_op jit(solution)/shard_map/all_gather | solution.py:44
  7.9 60.8 %all-gather.6.cloned.1.call-start = ((), (), s32[]{:S(2)}) async-start(), calls=%async_computation.2 | async-start | bytes 1769472 | tf_op jit(solution)/shard_map/all_gather | solution.py:54
  9.7 95.8 %reduce-scatter.2.cloned.1.call-start = ((), (), s32[]{:S(2)}) async-start(), calls=%async_computation.3 | async-start | bytes 1310720 | tf_op jit(solution)/shard_map/reduce_scatter | solution.py:63
  23.1 2.8 %copy-start.2 = (bf16[256,128]{1,0:T(8,128)(2,1)S(1)}, bf16[256,128]{1,0:T(8,128)(2,1)}, u32[]{:S(2)}) copy-start(bf16[256,128]{1,0:T(8,128)(2,1)} %param.9) | copy-start | bytes 196612
  76.6 1.5 %copy-start.3 = (bf16[256]{0:T(256)(128)(2,1)S(1)}, bf16[256]{0:T(256)(128)(2,1)}, u32[]{:S(2)}) copy-start(bf16[256]{0:T(256)(128)(2,1)} %param.11) | copy-start | bytes 1540
  76.6 28.9 %copy-start.1 = (bf16[512,256]{1,0:T(8,128)(2,1)S(1)}, bf16[512,256]{1,0:T(8,128)(2,1)}, u32[]{:S(2)}) copy-start(bf16[512,256]{1,0:T(8,128)(2,1)} %param.6) | copy-start | bytes 786436
  106.6 10.3 %copy-start = (bf16[512,256]{1,0:T(8,128)(2,1)}, bf16[512,256]{1,0:T(8,128)(2,1)S(1)}, u32[]{:S(2)}) copy-start(bf16[512,256]{1,0:T(8,128)(2,1)S(1)} %add_convert_fusion) | copy-start | bytes 786436
Sparse Core Ops, SparseCore 0:
  9.5 32.5 all-gather.3
  44.6 24.0 all-gather.5
  78.2 27.2 reduce-scatter.1
where the time goes:
time: 124 us; the launch traced here: 123 us
  waiting for transfers between devices  59.4 us (48%)
  blocking collectives  31.9 us (26%)
  between operations  13.8 us (11%)
  matrix products  8.6 us (7%)
  local copies, waits for them, and re-layouts  6 us (5%)
  other arithmetic  3.54 us (3%)
    reduce_scatter x1, waiting for transfers between devices, on_device(): lax.psum_scatter(partial_value.astype(jnp.bfloat16), 'mp', scatter_dimens...  27.4 us
    all_gather x1, waiting for transfers between devices, on_device(): lax.all_gather(input_weight, 'dp', axis=1, tiled=True)  25.1 us
    all_gather x1, blocking collectives, on_device(): lax.all_gather(pre_gain, 'mp', axis=0, tiled=True)  12.6 us
    all_gather x1, blocking collectives, on_device(): lax.all_gather(output_weight, 'dp', axis=1, tiled=True)  9.99 us
    psum x1, blocking collectives, on_device(): squares = lax.psum(jnp.sum(restored * restored, axis=1), 'mp')  9.28 us
    all_gather x1, waiting for transfers between devices, on_device(): lax.all_gather(tokens, 'mp', axis=1, tiled=True)  6.23 us
    unnamed x11, local copies, waits for them, and re-layouts  5.24 us
    dot_general x1, matrix products, one_sequence(): jnp.einsum('hqk,khd->qhd', probabilities, sequence_block[2], preferred_el...  2.86 us
  transfers between devices with their start and end apart: 3, of which 3 were waited for; matrix products, arithmetic and copies ran while one was open for 5% of the time, Pallas kernels for 0%

commit v1 on v0

--- a/solution.py
+++ b/solution.py
@@ -4,6 +4,22 @@
 from jax.sharding import PartitionSpec as P
 
 epsilon = 1e-06
+
+
+def summed_both_ways(shard, axis, dim, term):
+    count, index, span = (lax.axis_size(axis), lax.axis_index(axis), shard.shape[dim])
+    right = [(i, (i + 1) % count) for i in range(count)]
+    left = [(i, (i - 1) % count) for i in range(count)]
+    halfway = count // 2
+    from_left = from_right = shard
+    total = term(shard, index * span)
+    for hop in range(1, halfway + 1):
+        from_left = lax.ppermute(from_left, axis, right)
+        if hop < count - halfway:
+            from_right = lax.ppermute(from_right, axis, left)
+            total = total + term(from_right, (index + hop) % count * span)
+        total = total + term(from_left, (index - hop) % count * span)
+    return total
 
 
 def attend_all(mixed_heads, position_bias):
@@ -48,11 +64,16 @@
     inverse_rms = lax.rsqrt(jnp.mean(widened * widened, axis=1, keepdims=True) + epsilon)
     normed_in = (widened * inverse_rms * gain_all.astype(jnp.float32)).astype(jnp.bfloat16)
     feature_count = tokens.shape[1]
-    projected = jnp.einsum(
-        "td,kdi->kti",
-        normed_in,
-        lax.all_gather(input_weight, "dp", axis=1, tiled=True),
-        preferred_element_type=jnp.float32,
+    projected = summed_both_ways(
+        input_weight,
+        "dp",
+        1,
+        lambda part, offset: jnp.einsum(
+            "td,kdi->kti",
+            lax.dynamic_slice_in_dim(normed_in, offset, part.shape[1], axis=1),
+            part,
+            preferred_element_type=jnp.float32,
+        ),
     )
     context = attend_all(projected.astype(jnp.bfloat16), position_bias)
     partial_value = jnp.dot(

time: 124 us -> 114 us (0.919)
  waiting for transfers between devices: 59.4 us -> 33.1 us
  starting transfers between devices: 0.12 us -> 7.87 us
  matrix products: 8.6 us -> 12.8 us
  blocking collectives: 31.9 us -> 35 us
  other arithmetic: 3.54 us -> 5.07 us
    all_gather x1 -> x0, waiting for transfers between devices: 25.1 us -> none  [on_device(): lax.all_gather(input_weight, 'dp', axis=1, tiled=True)]
    ppermute x0 -> x7, starting transfers between devices: none -> 7.8 us  [the longest x3 7.2 us: summed_both_ways(): from_right = lax.ppermute(from_right, axis, left)]
    ppermute x0 -> x7, waiting for transfers between devices: none -> 6.58 us  [the longest x4 5.65 us: summed_both_ways(): from_left = lax.ppermute(from_left, axis, right)]
    all_gather x1, waiting for transfers between devices: 6.23 us -> 0.01 us  [on_device(): lax.all_gather(tokens, 'mp', axis=1, tiled=True)]
    dot_general x1 -> x8, matrix products: 2.82 us -> 7.06 us  [on_device(): jnp.einsum('td,kdi->kti', lax.dynamic_slice_in_dim(normed_in, offset, par...]
    all_gather x1, blocking collectives: 9.99 us -> 12.7 us  [on_device(): lax.all_gather(output_weight, 'dp', axis=1, tiled=True)]
    reduce_scatter x1, waiting for transfers between devices: 27.4 us -> 25.9 us  [on_device(): lax.psum_scatter(partial_value.astype(jnp.bfloat16), 'mp', scatter_dimens...]
    convert_element_type x0 -> x1, other arithmetic: none -> 1.53 us  [on_device(): (widened * inverse_rms * gain_all.astype(jnp.float32)).astype(jnp.bfloat16)]
  transfers between devices with their start and end apart: 3 -> 9, of which waited for: 3 -> 4; matrix products, arithmetic and copies ran while one was open for 5% -> 12% of each run, Pallas kernels for 0% -> 0%
where the time goes in v1:
time: 114 us
  blocking collectives  35 us (31%)
  waiting for transfers between devices  33.1 us (29%)
  between operations  14.3 us (13%)
  matrix products  12.8 us (11%)
  starting transfers between devices  7.87 us (7%)
  local copies, waits for them, and re-layouts  5.35 us (5%)
  other arithmetic  5.07 us (4%)
    reduce_scatter x1, waiting for transfers between devices, on_device(): lax.psum_scatter(partial_value.astype(jnp.bfloat16), 'mp', scatter_dimens...  25.9 us
    all_gather x1, blocking collectives, on_device(): lax.all_gather(pre_gain, 'mp', axis=0, tiled=True)  13 us
    all_gather x1, blocking collectives, on_device(): lax.all_gather(output_weight, 'dp', axis=1, tiled=True)  12.7 us
    psum x1, blocking collectives, on_device(): squares = lax.psum(jnp.sum(restored * restored, axis=1), 'mp')  9.26 us
    ppermute x3, starting transfers between devices, summed_both_ways(): from_right = lax.ppermute(from_right, axis, left)  7.2 us
    dot_general x8, matrix products, on_device(): jnp.einsum('td,kdi->kti', lax.dynamic_slice_in_dim(normed_in, offset, par...  7.06 us
    ppermute x4, waiting for transfers between devices, summed_both_ways(): from_left = lax.ppermute(from_left, axis, right)  5.65 us
    unnamed x13, local copies, waits for them, and re-layouts  4.6 us
  transfers between devices with their start and end apart: 9, of which 4 were waited for; matrix products, arithmetic and copies ran while one was open for 12% of the time, Pallas kernels for 0%

profile of v1, /device:TPU:0, one launch (start us, length us, event | category | flops | bytes accessed | tf_op | source)
XLA Modules:
  0.0 113.5 jit_solution(754326572784996511)
XLA Ops:
  7.2 0.0 all-gather.3.cloned.1.call-start
  7.2 0.7 all-gather.3.cloned.1.call-update
  7.9 0.0 reduce-scatter.2.cloned.1.call-start
  7.9 1.1 copy.14
  9.0 0.5 collective-permute-start.1
  9.6 2.9 %collective-permute-start = (bf16[3,128,256]{1,2,0:T(8,128)(2,1)S(1)}, bf16[3,128,256]{1,2,0:T(8,128)(2,1)S(1)}, u32[]{:S(2)}, u32[]{:S(2)}) collective-permute-start(bf16[3,128,256]{1,2,0:T(8,128)(2,1)S(1)} %copy.14), channel_id=1, source_target_pairs={{0,28},{4,0},{8,4},{12,8},{16,12},{20,16},{24,20},{28,24},{1,29},{... | collective-permute-start | bytes 589832 | tf_op jit(solution)/shard_map/ppermute | solution.py:19
  12.5 3.3 %collective-permute-done.1 = bf16[3,128,256]{1,2,0:T(8,128)(2,1)S(1)} collective-permute-done((bf16[3,128,256]{1,2,0:T(8,128)(2,1)S(1)}, bf16[3,128,256]{1,2,0:T(8,128)(2,1)S(1)}, u32[]{:S(2)}, u32[]{:S(2)}) %collective-permute-start.1) | collective-permute-done | bytes 196640 | tf_op jit(solution)/shard_map/ppermute | solution.py:17
  15.8 0.1 collective-permute-start.3
  15.9 0.9 collective-permute-done
  16.8 2.8 %collective-permute-start.2 = (bf16[3,128,256]{1,2,0:T(8,128)(2,1)S(1)}, bf16[3,128,256]{1,2,0:T(8,128)(2,1)S(1)}, u32[]{:S(2)}, u32[]{:S(2)}) collective-permute-start(bf16[3,128,256]{1,2,0:T(8,128)(2,1)S(1)} %collective-permute-done), channel_id=1, source_target_pairs={{0,28},{4,0},{8,4},{12,8},{16,12},{20,16},{24,20},{28,24},{1,29},{... | collective-permute-start | bytes 589832 | tf_op jit(solution)/shard_map/ppermute | solution.py:19
  19.6 2.4 %collective-permute-done.3 = bf16[3,128,256]{1,2,0:T(8,128)(2,1)} collective-permute-done((bf16[3,128,256]{1,2,0:T(8,128)(2,1)S(1)}, bf16[3,128,256]{1,2,0:T(8,128)(2,1)}, u32[]{:S(2)}, u32[]{:S(2)}) %collective-permute-start.3) | collective-permute-done | bytes 196640 | tf_op jit(solution)/shard_map/ppermute | solution.py:17
  21.9 0.0 collective-permute-start.5
  21.9 0.7 reshape.34
  22.6 13.0 %all-gather = bf16[4,1,256]{2,1,0:T(2,128)(2,1)S(1)} all-gather(bf16[1,1,256]{2,1,0:T(2,128)(2,1)S(1)} %reshape.34), channel_id=1, replica_groups=mesh['dp'=8,'mp'=4] {'mp'}, dimensions={0}, use_global_device_ids=true | all-gather | bytes 2560 | tf_op jit(solution)/shard_map/all_gather | solution.py:61
  35.6 0.0 copy-start.3
  35.6 2.8 %copy.16 = bf16[4,512,512]{1,2,0:T(8,128)(2,1)S(1)} copy(bf16[4,512,512]{2,1,0:T(8,128)(2,1)} %param.10) | data formatting | bytes 4194304 | tf_op args[4]
  38.5 0.0 copy-start.2
  38.5 0.0 copy-done.3
  38.5 12.7 %all_gather.11 = bf16[256,1024]{1,0:T(8,128)(2,1)S(1)} all-gather(bf16[256,128]{1,0:T(8,128)(2,1)S(1)} %copy-done.3), channel_id=1, replica_groups=mesh['dp'=8,'mp'=4] {'dp'}, dimensions={1}, use_global_device_ids=true | all-gather | bytes 589824 | tf_op jit(solution)/shard_map/all_gather | solution.py:81
  51.2 0.0 collective-permute-done.2
  51.2 1.5 %collective-permute-start.4 = (bf16[3,128,256]{1,2,0:T(8,128)(2,1)S(1)}, bf16[3,128,256]{1,2,0:T(8,128)(2,1)}, u32[]{:S(2)}, u32[]{:S(2)}) collective-permute-start(bf16[3,128,256]{1,2,0:T(8,128)(2,1)S(1)} %collective-permute-done.2), channel_id=1, source_target_pairs={{0,28},{4,0},{8,4},{12,8},{16,12},{20,16},{24,20},{28,24},{1,29},{... | collective-permute-start | bytes 589832 | tf_op jit(solution)/shard_map/ppermute | solution.py:19
  52.7 0.0 collective-permute-done.5
  52.7 0.0 collective-permute-start.6
  52.7 0.0 all-gather.3.cloned.1.call-done
  52.7 1.5 %fusion.2 = f32[512]{0:T(512)S(1)} fusion(bf16[512,1024]{1,0:T(8,128)(2,1)} %all-gather.3.cloned.1.call-done), kind=kLoop, calls=%fused_computation.7 | loop fusion | flops 1572352 | bytes 1050624 | tf_op jit(solution)/shard_map/reduce_sum | solution.py:64
  54.2 1.5 %fusion.4 = bf16[512,1024]{1,0:T(8,128)(2,1)S(1)} fusion(bf16[512,1024]{1,0:T(8,128)(2,1)} %all-gather.3.cloned.1.call-done, f32[1024]{0:T(1024)S(1)} %bitcast.54, f32[512]{0:T(512)S(1)} %add_rsqrt_fusion.1), kind=kLoop, calls=%fused_computation.9 | loop fusion | flops 2097152 | bytes 2103296 | tf_op jit(solution)/shard_map/convert_element_type | solution.py:65
  55.8 0.0 copy-done.2
  55.8 0.4 fusion.26
  56.2 1.3 %fusion.14 = f32[512,3,256]{0,2,1:T(8,128)S(1)} fusion(bf16[3,128,256]{1,2,0:T(8,128)(2,1)} %collective-permute-done.5, bf16[512,1024]{1,0:T(8,128)(2,1)S(1)} %fusion.4, s32[]{:T(128)S(6)} %select_n.70), kind=kOutput, calls=%fused_computation.23 | convolution fusion | flops 100663296 | bytes 1900548 | tf_op jit(solution)/shard_map/td,kdi->kti/dot_general | solution.py:71
  57.5 1.3 %fusion.18 = f32[512,3,256]{0,2,1:T(8,128)S(1)} fusion(bf16[3,128,256]{1,2,0:T(8,128)(2,1)} %collective-permute-done.3, bf16[512,1024]{1,0:T(8,128)(2,1)S(1)} %fusion.4, s32[]{:T(128)S(6)} %select_n.66), kind=kOutput, calls=%fused_computation.27 | convolution fusion | flops 100663296 | bytes 1900548 | tf_op jit(solution)/shard_map/td,kdi->kti/dot_general | solution.py:71
  58.8 0.4 fusion.20
  59.2 0.4 fusion.22
  59.6 0.4 fusion.24
  60.0 0.0 collective-permute-done.4
  60.0 1.3 %fusion.16 = f32[512,3,256]{0,2,1:T(8,128)S(1)} fusion(bf16[3,128,256]{1,2,0:T(8,128)(2,1)} %collective-permute-done.4, bf16[512,1024]{1,0:T(8,128)(2,1)S(1)} %fusion.4, s32[]{:T(128)S(6)} %select_n.68), kind=kOutput, calls=%fused_computation.25 | convolution fusion | flops 100663296 | bytes 1900548 | tf_op jit(solution)/shard_map/td,kdi->kti/dot_general | solution.py:71
  61.3 0.0 collective-permute-done.6
  61.3 1.6 %fusion.6 = bf16[3,512,256]{1,2,0:T(8,128)(2,1)S(1)} fusion(bf16[3,128,256]{1,2,0:T(8,128)(2,1)} %collective-permute-done.6, f32[512,3,256]{0,2,1:T(8,128)S(1)} %fusion.14, f32[512,3,256]{0,2,1:T(8,128)S(1)} %fusion.16, f32[512,3,256]{0,2,1:T(8,128)S(1)} %fusion.18, f32[512,3,256]{0,2,1:T(8,128)S(1)} %fusion.20, f32[512,3,256]{0,2,1:T(8,128)S(1)} %fusion.22, ...), kind=kOutput, calls=%fused_computation.13 | convolution fusion | flops 103809024 | bytes 12124164 | tf_op jit(solution)/shard_map/td,kdi->kti/dot_general | solution.py:71
  62.9 0.8 fusion.45
  63.7 1.5 %fusion.46 = f32[4,512]{1,0:T(4,128)S(1)} fusion(bf16[4,512,512]{1,2,0:T(8,128)(2,1)S(1)} %copy.16, bf16[512,4,64]{0,2,1:T(8,128)(2,1)S(1)} %bitcast.51, bf16[512,4,64]{0,2,1:T(8,128)(2,1)S(1)} %bitcast.49), kind=kOutput, calls=%fused_computation.57 | convolution fusion | flops 138412544 | bytes 2629632 | tf_op jit(solution)/shard_map/while/body/eval_jaxpr/sub | solution.py:47
  65.1 2.9 %fusion.7 = bf16[4,64,512]{2,1,0:T(8,128)(2,1)S(1)} fusion(bf16[512,4,64]{0,2,1:T(8,128)(2,1)} %bitcast.53, f32[4,512]{1,0:T(4,128)S(1)} %fusion.46, bf16[4,512,512]{1,2,0:T(8,128)(2,1)S(1)} %copy.16, bf16[512,4,64]{0,2,1:T(8,128)(2,1)S(1)} %bitcast.52, bf16[512,4,64]{0,2,1:T(8,128)(2,1)S(1)} %bitcast.50), kind=kOutput, calls=%fused_computation.14 | convolution fusion | flops 273811968 | bytes 3153920 | tf_op jit(solution)/shard_map/while/body/eval_jaxpr/hqk,khd->qhd/dot_general | solution.py:49
  68.0 0.0 copy-start.4
  68.0 0.0 copy-start.1
  68.0 1.4 %convolution_convert_fusion = bf16[512,1024]{1,0:T(8,128)(2,1)} fusion(bf16[512,256]{0,1:T(8,128)(2,1)S(1)} %bitcast.48, bf16[256,1024]{1,0:T(8,128)(2,1)S(1)} %all_gather.11), kind=kOutput, calls=%fused_computation.12 | convolution fusion | flops 268959744 | bytes 1835008 | tf_op jit(solution)/shard_map/dot_general | solution.py:79
  69.5 0.0 reduce-scatter.2.cloned.1.call-update
  69.5 0.0 copy-done.4
  69.5 25.9 %reduce-scatter.2.cloned.1.call-done = bf16[512,256]{1,0:T(8,128)(2,1)} async-done(((bf16[512,1024]{1,0:T(8,128)(2,1)}), bf16[512,256]{1,0:T(8,128)(2,1)}) %reduce-scatter.2.cloned.1.call-update) | async-done | bytes 262160 | tf_op jit(solution)/shard_map/reduce_scatter | solution.py:84
  95.4 0.0 copy-done.1
  95.4 1.0 add_convert_fusion.1
  96.4 0.0 copy-start
  96.4 0.1 fusion.8
  96.6 9.3 %psum.7 = f32[512]{0:T(512)S(1)} all-reduce(f32[512]{0:T(512)S(1)} %fusion.8), channel_id=1, replica_groups=mesh['dp'=8,'mp'=4] {'mp'}, use_global_device_ids=true, to_apply=%region_5.6 | all-reduce | flops 512 | bytes 4096 | tf_op jit(solution)/shard_map/psum | solution.py:89
  105.8 0.8 fusion.10
  106.7 0.0 copy-done
  (4 shorter events, 0.0 us)
Async XLA Ops:
  7.2 45.5 %all-gather.3.cloned.1.call-start = ((), (), s32[]{:S(2)}) async-start(), calls=%async_computation.1 | async-start | bytes 1310720 | tf_op jit(solution)/shard_map/all_gather | solution.py:60
  7.9 87.5 %reduce-scatter.2.cloned.1.call-start = ((), (), s32[]{:S(2)}) async-start(), calls=%async_computation.2 | async-start | bytes 1310720 | tf_op jit(solution)/shard_map/reduce_scatter | solution.py:84
  9.0 6.8 %collective-permute-start.1 = (bf16[3,128,256]{1,2,0:T(8,128)(2,1)S(1)}, bf16[3,128,256]{1,2,0:T(8,128)(2,1)S(1)}, u32[]{:S(2)}, u32[]{:S(2)}) collective-permute-start(bf16[3,128,256]{1,2,0:T(8,128)(2,1)S(1)} %copy.14), channel_id=1, source_target_pairs={{0,4},{4,8},{8,12},{12,16},{16,20},{20,24},{24,28},{28,0},{1,5},{5... | collective-permute-start | bytes 589832 | tf_op jit(solution)/shard_map/ppermute | solution.py:17
  9.6 7.2 %collective-permute-start = (bf16[3,128,256]{1,2,0:T(8,128)(2,1)S(1)}, bf16[3,128,256]{1,2,0:T(8,128)(2,1)S(1)}, u32[]{:S(2)}, u32[]{:S(2)}) collective-permute-start(bf16[3,128,256]{1,2,0:T(8,128)(2,1)S(1)} %copy.14), channel_id=1, source_target_pairs={{0,28},{4,0},{8,4},{12,8},{16,12},{20,16},{24,20},{28,24},{1,29},{... | collective-permute-start | bytes 589832 | tf_op jit(solution)/shard_map/ppermute | solution.py:19
  15.8 6.1 %collective-permute-start.3 = (bf16[3,128,256]{1,2,0:T(8,128)(2,1)S(1)}, bf16[3,128,256]{1,2,0:T(8,128)(2,1)}, u32[]{:S(2)}, u32[]{:S(2)}) collective-permute-start(bf16[3,128,256]{1,2,0:T(8,128)(2,1)S(1)} %collective-permute-done.1), channel_id=1, source_target_pairs={{0,4},{4,8},{8,12},{12,16},{16,20},{20,24},{24,28},{28,0},{1,5},{5... | collective-permute-start | bytes 589832 | tf_op jit(solution)/shard_map/ppermute | solution.py:17
  16.8 34.5 %collective-permute-start.2 = (bf16[3,128,256]{1,2,0:T(8,128)(2,1)S(1)}, bf16[3,128,256]{1,2,0:T(8,128)(2,1)S(1)}, u32[]{:S(2)}, u32[]{:S(2)}) collective-permute-start(bf16[3,128,256]{1,2,0:T(8,128)(2,1)S(1)} %collective-permute-done), channel_id=1, source_target_pairs={{0,28},{4,0},{8,4},{12,8},{16,12},{20,16},{24,20},{28,24},{1,29},{... | collective-permute-start | bytes 589832 | tf_op jit(solution)/shard_map/ppermute | solution.py:19
  21.9 30.8 %collective-permute-start.5 = (bf16[3,128,256]{1,2,0:T(8,128)(2,1)}, bf16[3,128,256]{1,2,0:T(8,128)(2,1)}, u32[]{:S(2)}, u32[]{:S(2)}) collective-permute-start(bf16[3,128,256]{1,2,0:T(8,128)(2,1)} %collective-permute-done.3), channel_id=1, source_target_pairs={{0,4},{4,8},{8,12},{12,16},{16,20},{20,24},{24,28},{28,0},{1,5},{5... | collective-permute-start | bytes 589832 | tf_op jit(solution)/shard_map/ppermute | solution.py:17
  35.6 2.9 %copy-start.3 = (bf16[256,128]{1,0:T(8,128)(2,1)S(1)}, bf16[256,128]{1,0:T(8,128)(2,1)}, u32[]{:S(2)}) copy-start(bf16[256,128]{1,0:T(8,128)(2,1)} %param.9) | copy-start | bytes 196612
  38.5 17.3 %copy-start.2 = (bf16[3,128,256]{2,1,0:T(8,128)(2,1)S(1)}, bf16[3,128,256]{2,1,0:T(8,128)(2,1)}, u32[]{:S(2)}) copy-start(bf16[3,128,256]{2,1,0:T(8,128)(2,1)} %param.8) | copy-start | bytes 589828
  51.2 8.7 %collective-permute-start.4 = (bf16[3,128,256]{1,2,0:T(8,128)(2,1)S(1)}, bf16[3,128,256]{1,2,0:T(8,128)(2,1)}, u32[]{:S(2)}, u32[]{:S(2)}) collective-permute-start(bf16[3,128,256]{1,2,0:T(8,128)(2,1)S(1)} %collective-permute-done.2), channel_id=1, source_target_pairs={{0,28},{4,0},{8,4},{12,8},{16,12},{20,16},{24,20},{28,24},{1,29},{... | collective-permute-start | bytes 589832 | tf_op jit(solution)/shard_map/ppermute | solution.py:19
  52.7 8.6 %collective-permute-start.6 = (bf16[3,128,256]{1,2,0:T(8,128)(2,1)}, bf16[3,128,256]{1,2,0:T(8,128)(2,1)}, u32[]{:S(2)}, u32[]{:S(2)}) collective-permute-start(bf16[3,128,256]{1,2,0:T(8,128)(2,1)} %collective-permute-done.5), channel_id=1, source_target_pairs={{0,4},{4,8},{8,12},{12,16},{16,20},{20,24},{24,28},{28,0},{1,5},{5... | collective-permute-start | bytes 589832 | tf_op jit(solution)/shard_map/ppermute | solution.py:17
  68.0 1.5 %copy-start.4 = (bf16[256]{0:T(256)(128)(2,1)S(1)}, bf16[256]{0:T(256)(128)(2,1)}, u32[]{:S(2)}) copy-start(bf16[256]{0:T(256)(128)(2,1)} %param.11) | copy-start | bytes 1540
  68.0 27.4 %copy-start.1 = (bf16[512,256]{1,0:T(8,128)(2,1)S(1)}, bf16[512,256]{1,0:T(8,128)(2,1)}, u32[]{:S(2)}) copy-start(bf16[512,256]{1,0:T(8,128)(2,1)} %param.6) | copy-start | bytes 786436
  96.4 10.3 %copy-start = (bf16[512,256]{1,0:T(8,128)(2,1)}, bf16[512,256]{1,0:T(8,128)(2,1)S(1)}, u32[]{:S(2)}) copy-start(bf16[512,256]{1,0:T(8,128)(2,1)S(1)} %add_convert_fusion.1) | copy-start | bytes 786436
Sparse Core Ops, SparseCore 0:
  9.5 32.7 all-gather.2
  69.6 25.7 reduce-scatter.1
